TPU v7x, 32 devices: a whole 2x2x4 slice. The times are simulated.
32 devices in a mesh: outer: 4 (over y, x), inner: 8 (over z, core).
Axes of the slice: x: 2, y: 2, z: 4, core: 2. Of those that a mesh axis runs over, the one named last changes fastest.
Arguments:
- tokens: bfloat16 [4096, 4096], P('inner', 'outer'), may hold values from -6 to 6
- cotangent: bfloat16 [4096, 4096], P('inner', 'outer'), may hold values from -0.09375 to 0.09375
- weight_cache: bfloat16 [4096, 4096], P(None, 'outer'), may hold values from -0.09375 to 0.09375
- weight_delta: bfloat16 [4096, 4096], P('inner', 'outer'), may hold values from -0.078125 to 0.078125
- sign_bits: int32 [4096], P('outer'), may hold values from 0 to 1
- master: float32 [4096, 4096], P('inner', 'outer'), may hold values from -1.5 to 1.5
- moment: float32 [4096, 4096], P('inner', 'outer'), may hold values from -6 to 6
- variance: float32 [4096, 4096], P('inner', 'outer'), may hold values from 0.25 to 4
Outputs:
- activation: float32 [4096, 4096], P('inner', 'outer')
- new_master: float32 [4096, 4096], P('inner', 'outer')
- new_moment: float32 [4096, 4096], P('inner', 'outer')
- new_variance: float32 [4096, 4096], P('inner', 'outer')
- block_scales: float32 [4096, 32], P('inner', 'outer')
All inputs are finite; a program needn't handle non-finite values.
Results may differ from a plain program's by a relative error of at most 0.003.
Values may be sent and summed in bfloat16 or wider, within the bound.
No kernel may reach another device: no remote copies, remote signals or barrier semaphores. Data moves between devices by JAX's collectives and lax.ppermute only.
A program may use at most 128 MiB of HBM per device.

v0:
```python
import jax
import jax.numpy as jnp
from jax import lax
from jax.sharding import PartitionSpec as P

BLOCK = 128


def hadamard_table(length):
    first = jnp.arange(length, dtype=jnp.int32)[:, None]
    second = jnp.arange(length, dtype=jnp.int32)[None, :]
    common = jnp.bitwise_and(first, second)
    parity = jnp.zeros((length, length), jnp.int32)
    for place in range(length.bit_length() - 1):
        parity = parity + jnp.bitwise_and(jnp.right_shift(common, place), 1)
    return (1 - 2 * (parity % 2)).astype(jnp.float32) / jnp.sqrt(jnp.float32(length))


def smooth(values, signs, table):
    height = values.shape[0]
    blocks = values.reshape(height, -1, table.shape[0]) * signs.reshape(-1, table.shape[0])
    mixed = jnp.einsum("rbk,kj->rbj", blocks, table, precision=lax.Precision.HIGHEST)
    return mixed.reshape(height, -1)


def unsmooth(values, signs, table):
    height = values.shape[0]
    blocks = values.reshape(height, -1, table.shape[0])
    mixed = jnp.einsum("rbj,jk->rbk", blocks, table, precision=lax.Precision.HIGHEST)
    return (mixed * signs.reshape(-1, table.shape[0])).reshape(height, -1)


def outer_product(left, right):
    return lax.dot_general(
        left, right, (((0,), (0,)), ((), ())), preferred_element_type=jnp.float32
    )


def body(tokens, cotangent, weight_cache, weight_delta, sign_bits, master, moment, variance):
    table = hadamard_table(BLOCK)
    signs = (1 - 2 * sign_bits).astype(jnp.float32)
    shard_rows = master.shape[0]
    gathered = lax.all_gather(tokens, "outer", axis=1, tiled=True)
    merged = (
        weight_cache.astype(jnp.float32)
        + lax.all_gather(weight_delta, "inner", axis=0, tiled=True).astype(jnp.float32)
    ).astype(jnp.bfloat16)
    columns = gathered
    output = jnp.dot(columns, merged, preferred_element_type=jnp.float32)
    columns = gathered
    partial_value = outer_product(columns, cotangent)
    summed = lax.psum_scatter(
        smooth(partial_value, signs, table), "inner", scatter_dimension=0, tiled=True
    )
    block_scales = jnp.max(jnp.abs(summed.reshape(shard_rows, -1, BLOCK)), axis=2)
    restored = unsmooth(summed, signs, table)
    new_moment = 0.9 * moment + 0.1 * restored
    new_variance = 0.95 * variance + 0.05 * restored * restored
    corrected = new_moment / (1.0 - 0.9**10)
    spread = jnp.sqrt(new_variance / (1.0 - 0.95**10)) + 1e-08
    new_master = master - 0.01 * (corrected / spread + 0.1 * master)
    return (output, new_master, new_moment, new_variance, block_scales)


def solution(mesh):
    placed = (
        P("inner", "outer"),
        P("inner", "outer"),
        P(None, "outer"),
        P("inner", "outer"),
        P("outer"),
        P("inner", "outer"),
        P("inner", "outer"),
        P("inner", "outer"),
    )
    return jax.shard_map(
        body,
        mesh=mesh,
        in_specs=placed,
        out_specs=(
            P("inner", "outer"),
            P("inner", "outer"),
            P("inner", "outer"),
            P("inner", "outer"),
            P("inner", "outer"),
        ),
        check_vma=False,
    )
```

profile of v0, /device:TPU:0, one launch (start us, length us, event | category | flops | bytes accessed | tf_op | source)
XLA Modules:
  0.0 339.3 jit_solution(2101183331217404971)
XLA Ops:
  7.2 0.0 copy-start
  7.2 0.0 copy-start.3
  7.2 0.0 all-gather.5.cloned.1.call-start
  7.2 0.7 all-gather.5.cloned.1.call-update
  7.9 0.0 all-gather.3.cloned.1.call-start
  8.0 0.7 all-gather.3.cloned.1.call-update
  8.7 0.0 reduce-scatter.2.cloned.1.call-start
  8.7 0.0 copy-done.3
  8.7 56.4 %all-gather.5.cloned.1.call-done = bf16[512,4096]{1,0:T(8,128)(2,1)} async-done(((bf16[512,1024]{1,0:T(8,128)(2,1)}), bf16[512,4096]{1,0:T(8,128)(2,1)}) %all-gather.5.cloned.1.call-update) | async-done | bytes 4194320 | tf_op jit(solution)/shard_map/all_gather | solution.py:43
  65.2 0.0 copy-done
  65.2 11.0 %fusion.47 = f32[4096,1024]{0,1:T(8,128)} fusion(bf16[512,4096]{1,0:T(8,128)(2,1)} %all-gather.5.cloned.1.call-done, bf16[512,1024]{1,0:T(8,128)(2,1)S(1)} %copy-done), kind=kOutput, calls=%fused_computation.54 | convolution fusion | flops 4294967296 | bytes 22020096 | tf_op jit(solution)/shard_map/dot_general | solution.py:34
  76.2 17.8 %copy.18 = f32[4096,8,128]{2,0,1:T(8,128)} copy(f32[4096,8,128]{0,2,1:T(8,128)} %bitcast.18) | data formatting | bytes 33554432 | tf_op jit(solution)/shard_map/reshape | solution.py:21
  93.9 22.9 %fusion = f32[4096,8,128]{0,2,1:T(8,128)} fusion(f32[4096,8,128]{2,0,1:T(8,128)} %copy.18, f32[8,128]{1,0:T(8,128)S(1)} %convert_bitcast_fusion), kind=kOutput, calls=%fused_computation | convolution fusion | flops 6447235072 | bytes 33558528 | tf_op jit(solution)/shard_map/rbk,kj->rbj/dot_general | solution.py:22
  116.9 0.0 reduce-scatter.2.cloned.1.call-update
  116.9 31.9 %all-gather.3.cloned.1.call-done = bf16[4096,1024]{1,0:T(8,128)(2,1)} async-done(((bf16[512,1024]{1,0:T(8,128)(2,1)}), bf16[4096,1024]{1,0:T(8,128)(2,1)}) %all-gather.3.cloned.1.call-update) | async-done | bytes 8388624 | tf_op jit(solution)/shard_map/all_gather | solution.py:46
  148.8 9.6 %fusion.5 = f32[512,1024]{0,1:T(8,128)S(1)} fusion(bf16[512,4096]{1,0:T(8,128)(2,1)} %all-gather.5.cloned.1.call-done, bf16[4096,1024]{1,0:T(8,128)(2,1)} %all-gather.3.cloned.1.call-done, bf16[4096,1024]{1,0:T(8,128)(2,1)} %param.10), kind=kOutput, calls=%fused_computation.10 | convolution fusion | flops 4311744512 | bytes 23068672 | tf_op jit(solution)/shard_map/dot_general | solution.py:49
  158.5 1.8 copy.23
  160.3 157.6 %reduce-scatter.2.cloned.1.call-done = f32[512,1024]{0,1:T(8,128)} async-done(((f32[4096,1024]{0,1:T(8,128)}), f32[512,1024]{0,1:T(8,128)}) %reduce-scatter.2.cloned.1.call-update) | async-done | bytes 2097168 | tf_op jit(solution)/shard_map/reduce_scatter | solution.py:52
  317.9 5.2 %convolution_multiply_fusion = f32[512,8,128]{0,2,1:T(8,128)} fusion(f32[512,8,128]{0,2,1:T(8,128)} %bitcast.19, f32[8,128]{1,0:T(8,128)S(1)} %convert_bitcast_fusion), kind=kOutput, calls=%fused_computation.11 | convolution fusion | flops 806420480 | bytes 4198400 | tf_op jit(solution)/shard_map/rbj,jk->rbk/dot_general | solution.py:29
  323.1 1.9 copy.20
  325.0 0.0 copy-start.2
  325.0 0.0 copy-start.1
  325.0 6.9 %multiply_subtract_fusion = (f32[512,1024]{1,0:T(8,128)}, f32[512,1024]{1,0:T(8,128)}, f32[512,1024]{1,0:T(8,128)}) fusion(f32[512,1024]{1,0:T(8,128)} %param.13, f32[512,1024]{1,0:T(8,128)S(1)} %copy.20, f32[512,1024]{1,0:T(8,128)} %param.14, f32[512,1024]{1,0:T(8,128)} %param.15), kind=kLoop, calls=%fused_computation.8 | loop fusion | flops 7864320 | bytes 14680064 | tf_op jit(solution)/shard_map/sub | solution.py:61
  331.9 0.9 abs_reduce_fusion
  (3 shorter events, 0.0 us)
Async XLA Ops:
  7.2 58.0 %copy-start = (bf16[512,1024]{1,0:T(8,128)(2,1)S(1)}, bf16[512,1024]{1,0:T(8,128)(2,1)}, u32[]{:S(2)}) copy-start(bf16[512,1024]{1,0:T(8,128)(2,1)} %param.9) | copy-start | bytes 3145732
  7.2 1.5 copy-start.3
  7.2 58.0 %all-gather.5.cloned.1.call-start = ((), (), s32[]{:S(2)}) async-start(), calls=%async_computation.2 | async-start | bytes 5242880 | tf_op jit(solution)/shard_map/all_gather | solution.py:43
  7.9 140.9 %all-gather.3.cloned.1.call-start = ((), (), s32[]{:S(2)}) async-start(), calls=%async_computation.1 | async-start | bytes 9437184 | tf_op jit(solution)/shard_map/all_gather | solution.py:46
  8.7 309.2 %reduce-scatter.2.cloned.1.call-start = ((), (), s32[]{:S(2)}) async-start(), calls=%async_computation.3 | async-start | bytes 18874368 | tf_op jit(solution)/shard_map/reduce_scatter | solution.py:52
  325.0 6.9 %copy-start.2 = (f32[512,1024]{0,1:T(8,128)S(1)}, f32[512,1024]{0,1:T(8,128)}, u32[]{:S(2)}) copy-start(f32[512,1024]{0,1:T(8,128)} %reduce-scatter.2.cloned.1.call-done) | copy-start | bytes 6291460
  325.0 7.8 %copy-start.1 = (bf16[512,1024]{1,0:T(8,128)(2,1)S(1)}, bf16[512,1024]{1,0:T(8,128)(2,1)}, u32[]{:S(2)}) copy-start(bf16[512,1024]{1,0:T(8,128)(2,1)} %param.9) | copy-start | bytes 3145732
Sparse Core Ops, SparseCore 0:
  9.8 55.2 all-gather.4
  66.8 82.0 all-gather.2
  151.2 166.6 reduce-scatter.1
where the time goes:
time: 340 us; the launch traced here: 339 us
  waiting for transfers between devices  247 us (73%)
  matrix products  48.7 us (14%)
  local copies, waits for them, and re-layouts  21.5 us (6%)
  between operations  13.8 us (4%)
  other arithmetic  7.74 us (2%)
    reduce_scatter x1, waiting for transfers between devices, body(): lax.psum_scatter(smooth(partial_value, signs, table), 'inner', scatter_di...  158 us
    all_gather x1, waiting for transfers between devices, body(): gathered = lax.all_gather(tokens, 'outer', axis=1, tiled=True)  56.4 us
    all_gather x1, waiting for transfers between devices, body(): lax.all_gather(weight_delta, 'inner', axis=0, tiled=True)  31.9 us
    dot_general x1, matrix products, smooth(): jnp.einsum('rbk,kj->rbj', blocks, table, precision=lax.Precision.HIGHEST)  22.9 us
    reshape x1, local copies, waits for them, and re-layouts, smooth(): values.reshape(height, -1, table.shape[0])  17.8 us
    dot_general x1, matrix products, outer_product(): lax.dot_general(left, right, (((0,), (0,)), ((), ())), preferred_element_...  11 us
    dot_general x1, matrix products, body(): output = jnp.dot(columns, merged, preferred_element_type=jnp.float32)  9.64 us
    sub x1, other arithmetic, body(): new_master = master - 0.01 * (corrected / spread + 0.1 * master)  6.87 us
  transfers between devices with their start and end apart: 3, of which 3 were waited for; matrix products, arithmetic and copies ran while one was open for 19% of the time, Pallas kernels for 0%

commit v1 on v0

--- a/solution.py
+++ b/solution.py
@@ -4,6 +4,19 @@
 from jax.sharding import PartitionSpec as P
 
 BLOCK = 128
+
+
+def ring_gather(x, axis, dim):
+    devices, index, span = (lax.axis_size(axis), lax.axis_index(axis), x.shape[dim])
+    right = [(i, (i + 1) % devices) for i in range(devices)]
+    out = jnp.zeros((*x.shape[:dim], devices * span, *x.shape[dim + 1 :]), x.dtype)
+    block = x
+    for step in range(devices):
+        owner = (index - step) % devices
+        out = lax.dynamic_update_slice_in_dim(out, block, owner * span, axis=dim)
+        if step < devices - 1:
+            block = lax.ppermute(block, axis, right)
+    return out
 
 
 def hadamard_table(length):
@@ -42,8 +55,7 @@
     shard_rows = master.shape[0]
     gathered = lax.all_gather(tokens, "outer", axis=1, tiled=True)
     merged = (
-        weight_cache.astype(jnp.float32)
-        + lax.all_gather(weight_delta, "inner", axis=0, tiled=True).astype(jnp.float32)
+        weight_cache.astype(jnp.float32) + ring_gather(weight_delta, "inner", 0).astype(jnp.float32)
     ).astype(jnp.bfloat16)
     columns = gathered
     output = jnp.dot(columns, merged, preferred_element_type=jnp.float32)

time: 340 us -> 392 us (1.15)
  waiting for transfers between devices: 247 us -> 292 us
  local copies, waits for them, and re-layouts: 21.5 us -> 31.1 us
    ppermute x0 -> x7, waiting for transfers between devices: none -> 235 us  [ring_gather(): block = lax.ppermute(block, axis, right)]
    reduce_scatter x1, waiting for transfers between devices: 158 us -> 0.01 us  [body(): lax.psum_scatter(smooth(partial_value, signs, table), 'inner', scatter_di...]
    all_gather x1 -> x0, waiting for transfers between devices: 31.9 us -> none  [body(): lax.all_gather(weight_delta, 'inner', axis=0, tiled=True)]
    unnamed x9 -> x23, local copies, waits for them, and re-layouts: 1.84 us -> 7.26 us
  transfers between devices with their start and end apart: 3 -> 9, of which waited for: 3 -> 8; matrix products, arithmetic and copies ran while one was open for 19% -> 4% of each run, Pallas kernels for 0% -> 0%
where the time goes in v1:
time: 392 us
  waiting for transfers between devices  292 us (74%)
  matrix products  45.4 us (12%)
  local copies, waits for them, and re-layouts  31.1 us (8%)
  between operations  14.2 us (4%)
  other arithmetic  8.43 us (2%)
    ppermute x7, waiting for transfers between devices, ring_gather(): block = lax.ppermute(block, axis, right)  235 us
    all_gather x1, waiting for transfers between devices, body(): gathered = lax.all_gather(tokens, 'outer', axis=1, tiled=True)  56.5 us
    dot_general x1, matrix products, smooth(): jnp.einsum('rbk,kj->rbj', blocks, table, precision=lax.Precision.HIGHEST)  22.8 us
    reshape x1, local copies, waits for them, and re-layouts, smooth(): values.reshape(height, -1, table.shape[0])  17.4 us
    dot_general x1, matrix products, outer_product(): lax.dot_general(left, right, (((0,), (0,)), ((), ())), preferred_element_...  10.3 us
  transfers between devices with their start and end apart: 9, of which 8 were waited for; matrix products, arithmetic and copies ran while one was open for 4% of the time, Pallas kernels for 0%

profile of v1, /device:TPU:0, one launch (start us, length us, event | category | flops | bytes accessed | tf_op | source)
XLA Modules:
  0.0 391.7 jit_solution(10975659063127363210)
XLA Ops:
  8.7 56.5 %all-gather.2.cloned.1.call-done = bf16[512,4096]{1,0:T(8,128)(2,1)} async-done(((bf16[512,1024]{1,0:T(8,128)(2,1)}), bf16[512,4096]{1,0:T(8,128)(2,1)}) %all-gather.2.cloned.1.call-update) | async-done | bytes 4194320 | tf_op jit(solution)/shard_map/all_gather | solution.py:56
  65.2 10.3 %fusion.47 = f32[4096,1024]{0,1:T(8,128)} fusion(bf16[512,4096]{1,0:T(8,128)(2,1)} %all-gather.2.cloned.1.call-done, bf16[512,1024]{1,0:T(8,128)(2,1)S(1)} %copy-done), kind=kOutput, calls=%fused_computation.62 | convolution fusion | flops 4294967296 | bytes 22020096 | tf_op jit(solution)/shard_map/dot_general | solution.py:47
  75.5 17.4 %copy.18 = f32[4096,8,128]{2,0,1:T(8,128)} copy(f32[4096,8,128]{0,2,1:T(8,128)} %bitcast.18) | data formatting | bytes 33554432 | tf_op jit(solution)/shard_map/reshape | solution.py:34
  92.9 22.8 %fusion = f32[4096,8,128]{0,2,1:T(8,128)} fusion(f32[4096,8,128]{2,0,1:T(8,128)} %copy.18, f32[8,128]{1,0:T(8,128)S(1)} %convert_bitcast_fusion), kind=kOutput, calls=%fused_computation | convolution fusion | flops 6447235072 | bytes 33558528 | tf_op jit(solution)/shard_map/rbk,kj->rbj/dot_general | solution.py:35
  115.7 1.2 copy-done.3
  116.9 30.4 %collective-permute-done = bf16[512,1024]{1,0:T(8,128)(2,1)S(1)} collective-permute-done((bf16[512,1024]{1,0:T(8,128)(2,1)S(1)}, bf16[512,1024]{1,0:T(8,128)(2,1)S(1)}, u32[]{:S(2)}, u32[]{:S(2)}) %collective-permute-start) | collective-permute-done | bytes 1048608 | tf_op jit(solution)/shard_map/ppermute | solution.py:18
  147.3 38.6 %collective-permute-done.1 = bf16[512,1024]{1,0:T(8,128)(2,1)S(1)} collective-permute-done((bf16[512,1024]{1,0:T(8,128)(2,1)S(1)}, bf16[512,1024]{1,0:T(8,128)(2,1)S(1)}, u32[]{:S(2)}, u32[]{:S(2)}) %collective-permute-start.1) | collective-permute-done | bytes 1048608 | tf_op jit(solution)/shard_map/ppermute | solution.py:18
  185.9 38.6 %collective-permute-done.2 = bf16[512,1024]{1,0:T(8,128)(2,1)S(1)} collective-permute-done((bf16[512,1024]{1,0:T(8,128)(2,1)S(1)}, bf16[512,1024]{1,0:T(8,128)(2,1)S(1)}, u32[]{:S(2)}, u32[]{:S(2)}) %collective-permute-start.2) | collective-permute-done | bytes 1048608 | tf_op jit(solution)/shard_map/ppermute | solution.py:18
  224.5 1.0 copy-done.4
  225.5 38.6 %collective-permute-done.3 = bf16[512,1024]{1,0:T(8,128)(2,1)S(1)} collective-permute-done((bf16[512,1024]{1,0:T(8,128)(2,1)S(1)}, bf16[512,1024]{1,0:T(8,128)(2,1)S(1)}, u32[]{:S(2)}, u32[]{:S(2)}) %collective-permute-start.3) | collective-permute-done | bytes 1048608 | tf_op jit(solution)/shard_map/ppermute | solution.py:18
  264.1 1.0 copy-done.6
  265.1 38.6 %collective-permute-done.4 = bf16[512,1024]{1,0:T(8,128)(2,1)S(1)} collective-permute-done((bf16[512,1024]{1,0:T(8,128)(2,1)S(1)}, bf16[512,1024]{1,0:T(8,128)(2,1)S(1)}, u32[]{:S(2)}, u32[]{:S(2)}) %collective-permute-start.4) | collective-permute-done | bytes 1048608 | tf_op jit(solution)/shard_map/ppermute | solution.py:18
  303.7 1.0 copy-done.8
  304.6 38.7 %collective-permute-done.5 = bf16[512,1024]{1,0:T(8,128)(2,1)} collective-permute-done((bf16[512,1024]{1,0:T(8,128)(2,1)S(1)}, bf16[512,1024]{1,0:T(8,128)(2,1)}, u32[]{:S(2)}, u32[]{:S(2)}) %collective-permute-start.5) | collective-permute-done | bytes 1048608 | tf_op jit(solution)/shard_map/ppermute | solution.py:18
  343.4 1.1 broadcast_in_dim.2
  344.8 0.9 copy-done.5
  346.5 1.5 constant_dynamic-update-slice_fusion.1
  348.0 11.7 %collective-permute-done.6 = bf16[512,1024]{1,0:T(8,128)(2,1)} collective-permute-done((bf16[512,1024]{1,0:T(8,128)(2,1)}, bf16[512,1024]{1,0:T(8,128)(2,1)}, u32[]{:S(2)}, u32[]{:S(2)}) %collective-permute-start.6) | collective-permute-done | bytes 1048608 | tf_op jit(solution)/shard_map/ppermute | solution.py:18
  359.7 1.3 constant_dynamic-update-slice_fusion
  361.0 7.1 %fusion.5 = f32[512,1024]{0,1:T(8,128)S(1)} fusion(bf16[512,4096]{1,0:T(8,128)(2,1)S(1)} %copy-done.10, bf16[4096,1024]{1,0:T(8,128)(2,1)S(1)} %constant_dynamic-update-slice_fusion, bf16[4096,1024]{1,0:T(8,128)(2,1)} %param.10), kind=kOutput, calls=%fused_computation.10 | convolution fusion | flops 4311744512 | bytes 23068672 | tf_op jit(solution)/shard_map/dot_general | solution.py:61
  368.2 1.8 copy.23
  370.0 5.2 %convolution_multiply_fusion = f32[512,8,128]{0,2,1:T(8,128)} fusion(f32[512,8,128]{0,2,1:T(8,128)} %bitcast.19, f32[8,128]{1,0:T(8,128)S(1)} %convert_bitcast_fusion), kind=kOutput, calls=%fused_computation.11 | convolution fusion | flops 806420480 | bytes 4198400 | tf_op jit(solution)/shard_map/rbj,jk->rbk/dot_general | solution.py:42
  375.2 1.9 copy.20
  377.1 6.9 %multiply_subtract_fusion = (f32[512,1024]{1,0:T(8,128)}, f32[512,1024]{1,0:T(8,128)}, f32[512,1024]{1,0:T(8,128)}) fusion(f32[512,1024]{1,0:T(8,128)} %param.13, f32[512,1024]{1,0:T(8,128)S(1)} %copy.20, f32[512,1024]{1,0:T(8,128)} %param.14, f32[512,1024]{1,0:T(8,128)} %param.15), kind=kLoop, calls=%fused_computation.8 | loop fusion | flops 7864320 | bytes 14680064 | tf_op jit(solution)/shard_map/sub | solution.py:73
  (37 shorter events, 3.5 us)
Async XLA Ops:
  7.2 58.0 %copy-start = (bf16[512,1024]{1,0:T(8,128)(2,1)S(1)}, bf16[512,1024]{1,0:T(8,128)(2,1)}, u32[]{:S(2)}) copy-start(bf16[512,1024]{1,0:T(8,128)(2,1)} %param.9) | copy-start | bytes 3145732
  7.2 58.0 %all-gather.2.cloned.1.call-start = ((), (), s32[]{:S(2)}) async-start(), calls=%async_computation.1 | async-start | bytes 5242880 | tf_op jit(solution)/shard_map/all_gather | solution.py:56
  7.9 362.1 %reduce-scatter.2.cloned.1.call-start = ((), (), s32[]{:S(2)}) async-start(), calls=%async_computation.2 | async-start | bytes 18874368 | tf_op jit(solution)/shard_map/reduce_scatter | solution.py:64
  115.7 1.2 copy-start.3
  116.9 30.4 %collective-permute-start = (bf16[512,1024]{1,0:T(8,128)(2,1)S(1)}, bf16[512,1024]{1,0:T(8,128)(2,1)S(1)}, u32[]{:S(2)}, u32[]{:S(2)}) collective-permute-start(bf16[512,1024]{1,0:T(8,128)(2,1)S(1)} %copy-done.3), channel_id=1, source_target_pairs={{0,1},{1,2},{2,3},{3,4},{4,5},{5,6},{6,7},{7,0},{8,9},{9,10},{10,1... | collective-permute-start | bytes 3145736 | tf_op jit(solution)/shard_map/ppermute | solution.py:18
  147.3 38.6 %collective-permute-start.1 = (bf16[512,1024]{1,0:T(8,128)(2,1)S(1)}, bf16[512,1024]{1,0:T(8,128)(2,1)S(1)}, u32[]{:S(2)}, u32[]{:S(2)}) collective-permute-start(bf16[512,1024]{1,0:T(8,128)(2,1)S(1)} %collective-permute-done), channel_id=1, source_target_pairs={{0,1},{1,2},{2,3},{3,4},{4,5},{5,6},{6,7},{7,0},{8,9},{9,10},{10,1... | collective-permute-start | bytes 3145736 | tf_op jit(solution)/shard_map/ppermute | solution.py:18
  185.9 38.6 %collective-permute-start.2 = (bf16[512,1024]{1,0:T(8,128)(2,1)S(1)}, bf16[512,1024]{1,0:T(8,128)(2,1)S(1)}, u32[]{:S(2)}, u32[]{:S(2)}) collective-permute-start(bf16[512,1024]{1,0:T(8,128)(2,1)S(1)} %collective-permute-done.1), channel_id=1, source_target_pairs={{0,1},{1,2},{2,3},{3,4},{4,5},{5,6},{6,7},{7,0},{8,9},{9,10},{10,1... | collective-permute-start | bytes 3145736 | tf_op jit(solution)/shard_map/ppermute | solution.py:18
  224.5 1.0 copy-start.4
  225.5 38.6 %collective-permute-start.3 = (bf16[512,1024]{1,0:T(8,128)(2,1)S(1)}, bf16[512,1024]{1,0:T(8,128)(2,1)S(1)}, u32[]{:S(2)}, u32[]{:S(2)}) collective-permute-start(bf16[512,1024]{1,0:T(8,128)(2,1)S(1)} %collective-permute-done.2), channel_id=1, source_target_pairs={{0,1},{1,2},{2,3},{3,4},{4,5},{5,6},{6,7},{7,0},{8,9},{9,10},{10,1... | collective-permute-start | bytes 3145736 | tf_op jit(solution)/shard_map/ppermute | solution.py:18
  264.1 1.0 copy-start.6
  265.1 38.6 %collective-permute-start.4 = (bf16[512,1024]{1,0:T(8,128)(2,1)S(1)}, bf16[512,1024]{1,0:T(8,128)(2,1)S(1)}, u32[]{:S(2)}, u32[]{:S(2)}) collective-permute-start(bf16[512,1024]{1,0:T(8,128)(2,1)S(1)} %collective-permute-done.3), channel_id=1, source_target_pairs={{0,1},{1,2},{2,3},{3,4},{4,5},{5,6},{6,7},{7,0},{8,9},{9,10},{10,1... | collective-permute-start | bytes 3145736 | tf_op jit(solution)/shard_map/ppermute | solution.py:18
  303.7 1.0 copy-start.8
  304.6 38.7 %collective-permute-start.5 = (bf16[512,1024]{1,0:T(8,128)(2,1)S(1)}, bf16[512,1024]{1,0:T(8,128)(2,1)}, u32[]{:S(2)}, u32[]{:S(2)}) collective-permute-start(bf16[512,1024]{1,0:T(8,128)(2,1)S(1)} %collective-permute-done.4), channel_id=1, source_target_pairs={{0,1},{1,2},{2,3},{3,4},{4,5},{5,6},{6,7},{7,0},{8,9},{9,10},{10,1... | collective-permute-start | bytes 3145736 | tf_op jit(solution)/shard_map/ppermute | solution.py:18
  343.4 16.3 %collective-permute-start.6 = (bf16[512,1024]{1,0:T(8,128)(2,1)}, bf16[512,1024]{1,0:T(8,128)(2,1)}, u32[]{:S(2)}, u32[]{:S(2)}) collective-permute-start(bf16[512,1024]{1,0:T(8,128)(2,1)} %collective-permute-done.5), channel_id=1, source_target_pairs={{0,1},{1,2},{2,3},{3,4},{4,5},{5,6},{6,7},{7,0},{8,9},{9,10},{10,1... | collective-permute-start | bytes 3145736 | tf_op jit(solution)/shard_map/ppermute | solution.py:18
  344.4 1.3 copy-start.5
  344.5 1.6 copy-start.7
  344.6 1.8 copy-start.9
  346.4 14.7 %copy-start.10 = (bf16[512,4096]{1,0:T(8,128)(2,1)S(1)}, bf16[512,4096]{1,0:T(8,128)(2,1)}, u32[]{:S(2)}) copy-start(bf16[512,4096]{1,0:T(8,128)(2,1)} %all-gather.2.cloned.1.call-done) | copy-start | bytes 12582916
  377.1 6.9 %copy-start.2 = (f32[512,1024]{0,1:T(8,128)S(1)}, f32[512,1024]{0,1:T(8,128)}, u32[]{:S(2)}) copy-start(f32[512,1024]{0,1:T(8,128)} %reduce-scatter.2.cloned.1.call-done) | copy-start | bytes 6291460
  377.1 7.8 %copy-start.1 = (bf16[512,1024]{1,0:T(8,128)(2,1)S(1)}, bf16[512,1024]{1,0:T(8,128)(2,1)}, u32[]{:S(2)}) copy-start(bf16[512,1024]{1,0:T(8,128)(2,1)} %param.9) | copy-start | bytes 3145732
Sparse Core Ops, SparseCore 0:
  9.8 55.2 all-gather.1
  115.8 232.2 reduce-scatter.1
